TPU v7x, 512 devices: a 4x2x32 block of a 4x16x32 slice. The times are simulated.
512 devices in a mesh: groups: 2 (over y), ctx: 32 (over z), head: 4 (over x), rep: 2 (over core).
Axes of the slice: x: 4, y: 2, z: 32, core: 2. Of those that a mesh axis runs over, the one named last changes fastest.
The devices are a block of a 4x16x32 slice.
Arguments:
- kv_cache: bfloat16 [4, 768, 128, 576], P(('groups', 'rep'), 'ctx'), parts along dimension 0, may hold values from -10 to 10
- queries: bfloat16 [4, 4, 128, 576], P(('groups', 'rep'), None, 'head'), parts along dimension 0, may hold values from -45 to 45
- new_latent: bfloat16 [4, 4, 576], P(('groups', 'rep')), parts along dimension 0, may hold values from -6 to 6
- page_counts: int32 [4, 4], P(('groups', 'rep')), parts along dimension 0, may hold values from 1 to 288, 576 in all within a row
- page_tails: int32 [4, 4], P(('groups', 'rep')), parts along dimension 0, may hold values from 1 to 128
- page_slots: int32 [4, 768], P(('groups', 'rep')), parts along dimension 0, may hold values from 0 to 767, each once within a row
Outputs:
- attended: bfloat16 [4, 4, 128, 512], P(('groups', 'rep'), None, 'head'), parts along dimension 0
There are 2 independent parts, one for each index of `groups`. A program takes and returns all parts, laid end to end along the dimension named above; each array names one. Nothing has to cross between parts.
Inputs may be any that keep to these rules, and one draw needn't show every extreme that they name: `page_counts`: the 4 counts of a half sum to 576, and the largest is exactly 288. `page_slots`: each half's row holds every slot once; only its first 576 entries are pages in use.
All inputs are finite; a program needn't handle non-finite values.
Results may differ from a plain program's by a relative error of at most 0.0033.
Values sent between devices are 32-bit elements; how exact they have to be, the bound alone decides.
No kernel may reach another device: no remote copies, remote signals or barrier semaphores. Data moves between devices by JAX's collectives and lax.ppermute only.
A program may use at most 64 MiB of HBM per device.

v0:
```python
import jax
import jax.numpy as jnp
from jax import lax
from jax.sharding import PartitionSpec as P

LATENT = 512


score_scale = 192.0 ** (-0.5)
neg_large = -1e30


def copy_for_each(shard, axis):
    size = lax.axis_size(axis)
    return lax.all_to_all(
        jnp.broadcast_to(shard[None], (size, *shard.shape)), axis, 0, 0, tiled=True
    )


def over_copies(shard, axis):
    everything = copy_for_each(shard, axis)
    return jnp.max(everything, axis=0)


def filled_up(lines, size):
    spare = -len(lines) % size
    return jnp.pad(lines, [(0, spare)] + [(0, 0)] * (lines.ndim - 1))


def laid_out(pieces, dim):
    pieces = jnp.moveaxis(pieces, 0, dim)
    lengths = pieces.shape
    return pieces.reshape(*lengths[:dim], lengths[dim] * lengths[dim + 1], *lengths[dim + 2 :])


def gather_directly(shard, axis, dim):
    return laid_out(copy_for_each(shard, axis), dim)


def cut_along(shard, dim, size):
    before, after = (shard.shape[:dim], shard.shape[dim + 1 :])
    return jnp.moveaxis(shard.reshape(*before, size, -1, *after), dim, 0)


def sent_and_summed(shard, axis, dim):
    pieces = cut_along(shard, dim, lax.axis_size(axis))
    arrived = lax.all_to_all(pieces, axis, split_axis=0, concat_axis=0, tiled=True)
    return arrived.sum(axis=0)


def sum_by_parts(shard, axes):
    padded = filled_up(shard, lax.axis_size(axes))
    whole = gather_directly(sent_and_summed(padded, axes, 0), axes, 0)
    return lax.slice_in_dim(whole, 0, len(shard)).reshape(shard.shape)


def together(arrays, axis):
    flat, at, done = (jnp.concatenate([a.reshape(-1) for a in arrays]), 0, [])
    so_far = sum_by_parts(flat, axis)
    for a in arrays:
        done.append(so_far[at : at + a.size].reshape(a.shape))
        at += a.size
    return tuple(done)


def page_layout(page_counts, page_tails, page_slots, pages_local, page_width):
    ctx_place = lax.axis_index("ctx")
    counts = page_counts[0]
    slot_ids = ctx_place * pages_local + jnp.arange(pages_local, dtype=jnp.int32)
    pack_rank = jnp.arange(page_slots.shape[1], dtype=jnp.int32)
    matches = page_slots[0][:, None] == slot_ids[None, :]
    page_rank = jnp.sum(jnp.where(matches, pack_rank[:, None], 0), axis=0)
    ends = jnp.cumsum(counts)
    starts = ends - counts
    page_live = page_rank < ends[-1]
    sequence_of = jnp.sum((ends[None, :] <= page_rank[:, None]).astype(jnp.int32), axis=1)
    sequence_of = jnp.minimum(sequence_of, counts.shape[0] - 1)
    page_number = page_rank - jnp.take(starts, sequence_of)
    lengths = (counts - 1) * page_width + page_tails[0]
    limit = jnp.take(lengths, sequence_of) - page_number * page_width
    token_place = jnp.arange(page_width, dtype=jnp.int32)
    token_valid = page_live[:, None] & (token_place[None, :] < limit[:, None])
    return (sequence_of, page_live, token_valid)


def page_partials(query_pages, cache_pages, token_valid):
    scores = (
        jnp.einsum("phc,ptc->pht", query_pages, cache_pages, preferred_element_type=jnp.float32)
        * score_scale
    )
    masked = jnp.where(token_valid[:, None, :], scores, neg_large)
    page_max = jnp.max(masked, axis=2)
    weights = jnp.where(
        token_valid[:, None, :], jnp.exp(masked - page_max[:, :, None]), 0.0
    ).astype(jnp.bfloat16)
    page_sum = jnp.sum(weights.astype(jnp.float32), axis=2)
    page_acc = jnp.einsum(
        "pht,ptc->phc", weights, cache_pages[:, :, :LATENT], preferred_element_type=jnp.float32
    )
    return (page_max, page_sum, page_acc)


def fold_pages(partials, owner, rows):
    page_max, page_sum, page_acc = partials
    member = owner[:, None] == jnp.arange(rows, dtype=jnp.int32)[None, :]
    row_max = jnp.max(jnp.where(member[:, :, None], page_max[:, None, :], neg_large), axis=0)
    owner_max = jnp.take(row_max, jnp.clip(owner, 0, rows - 1), axis=0)
    factor = jnp.where((owner >= 0)[:, None], jnp.exp(page_max - owner_max), 0.0)
    onehot = member.astype(jnp.float32)
    row_sum = jnp.einsum("ps,ph->sh", onehot, factor * page_sum, precision=lax.Precision.HIGHEST)
    row_acc = jnp.einsum(
        "ps,phc->shc", onehot, factor[:, :, None] * page_acc, precision=lax.Precision.HIGHEST
    )
    return (row_max, row_sum, row_acc)


def local(kv_cache, queries, new_latent, page_counts, page_tails, page_slots):
    pages_local = kv_cache.shape[1]
    page_width = kv_cache.shape[2]
    cache_pages = kv_cache[0]
    sequence_of, page_live, token_valid = page_layout(
        page_counts, page_tails, page_slots, pages_local, page_width
    )
    query_block = queries[0]
    batch_rows = query_block.shape[0]
    query_pages = jnp.take(query_block, sequence_of, axis=0)
    partials = page_partials(query_pages, cache_pages, token_valid)
    owner = jnp.where(page_live, sequence_of, -1)
    local_max, local_sum, local_acc = fold_pages(partials, owner, batch_rows)
    row_max = over_copies(local_max, "ctx")
    factor = jnp.exp(local_max - row_max)
    row_sum, row_acc = together((local_sum * factor, local_acc * factor[:, :, None]), "ctx")
    own_row = new_latent[0].astype(jnp.float32)
    own_score = (
        jnp.einsum("shc,sc->sh", query_block, new_latent[0], preferred_element_type=jnp.float32)
        * score_scale
    )
    top = jnp.maximum(row_max, own_score)
    keep_old = jnp.exp(row_max - top)
    own_factor = jnp.exp(own_score - top)
    numer = row_acc * keep_old[:, :, None] + own_factor[:, :, None] * own_row[:, None, :LATENT]
    denom = row_sum * keep_old + own_factor
    return (numer / denom[:, :, None]).astype(jnp.bfloat16)[None]


def solution(mesh):
    in_specs = (
        P(("groups", "rep"), "ctx", None, None),
        P(("groups", "rep"), None, "head", None),
        P(("groups", "rep"), None, None),
        P(("groups", "rep"), None),
        P(("groups", "rep"), None),
        P(("groups", "rep"), None),
    )
    out_specs = P(("groups", "rep"), None, "head", None)
    return jax.shard_map(local, mesh=mesh, in_specs=in_specs, out_specs=out_specs, check_vma=False)
```

profile of v0, /device:TPU:40, one launch (start us, length us, event | category | flops | bytes accessed | tf_op | source)
XLA Modules:
  0.0 187.0 jit_solution(13441541086064712017)
XLA Ops:
  0.0 0.0 copy-start
  0.0 0.7 reduce.1
  0.7 0.8 reduce-window.4
  1.6 0.6 slice.22
  2.2 0.2 select_reduce_fusion
  2.3 0.1 convert_reduce_fusion.1
  2.4 0.7 broadcast_compare_fusion
  3.1 0.7 bitcast_add_fusion
  3.8 0.7 fusion.42
  4.5 4.9 %fusion.30 = s32[24]{0:T(128)S(1)} fusion(s32[24]{0:T(128)S(1)} %select_reduce_fusion, s32[]{:T(128)} %bitcast.12, s32[]{:T(128)} %bitcast.11, s32[]{:T(128)} %bitcast.10, s32[]{:T(128)} %bitcast.9, s32[]{:T(128)} %bitcast.8, s32[]{:T(128)} %bitcast.7, s32[]{:T(128)} %bitcast.6, s32[]{:T(128)} %bitcast.5, s32[24]{0:T(128)S(1)} %convert_reduce_fusion.1), kind=kLoop, calls=%fused_computation.55 | loop fusion | flops 504 | bytes 320 | tf_op jit(solution)/shard_map/sub | solution.py:80
  9.4 0.1 fusion.22
  9.5 0.0 copy-done
  9.5 0.7 gather_fusion
  10.3 2.8 %fusion.44 = (f32[24,32]{1,0:T(8,128)S(1)}, f32[24,32,128]{2,1,0:T(8,128)S(1)}) fusion(bf16[1,24,128,576]{2,3,1,0:T(8,128)(2,1)} %param.8, bf16[24,32,576]{2,1,0:T(8,128)(2,1)S(1)} %gather_fusion, pred[24]{0:T(512)(128)(4,1)S(1)} %get-tuple-element.14, pred[24,128]{1,0:T(8,128)(4,1)S(1)} %fusion.22), kind=kOutput, calls=%fused_computation.75 | convolution fusion | flops 113982720 | bytes 4823064 | tf_op jit(solution)/shard_map/phc,ptc->pht/dot_general | solution.py:88
  13.1 0.1 select_reduce_fusion.1
  13.2 0.7 reshape.292
  13.9 45.8 %all-to-all-start = ((f32[32,1,128]{2,1,0:T(1,128)}), f32[32,1,128]{2,1,0:T(1,128)S(1)}, u32[]{:S(2)}, u32[]{:S(2)}) async-start(f32[32,1,128]{2,1,0:T(1,128)} %reshape.292), calls=%async_computation | async-start | bytes 32768 | tf_op jit(solution)/shard_map/all_to_all | solution.py:15
  59.7 6.1 %copy.25 = bf16[1,24,128,576]{3,2,1,0:T(8,128)(2,1)} copy(bf16[1,24,128,576]{2,3,1,0:T(8,128)(2,1)} %param.8) | data formatting | bytes 7077888 | tf_op args[0]
  65.8 0.6 gather_fusion.1
  66.4 0.1 exponential_select_fusion
  66.4 2.5 %fusion.6 = f32[24,32,512]{2,1,0:T(8,128)S(1)} fusion(bf16[24,128,576]{2,1,0:T(8,128)(2,1)} %bitcast.61, f32[24,32]{1,0:T(8,128)S(1)} %exponential_select_fusion, f32[24,32,128]{2,1,0:T(8,128)S(1)} %get-tuple-element.26, f32[24,32]{1,0:T(8,128)S(1)} %get-tuple-element.25, pred[24,128]{1,0:T(8,128)(4,1)S(1)} %fusion.22), kind=kOutput, calls=%fused_computation.8 | convolution fusion | flops 101351424 | bytes 5121024 | tf_op jit(solution)/shard_map/pht,ptc->phc/dot_general | solution.py:97
  69.0 0.3 convert_reduce_fusion
  69.3 12.0 %all-to-all-done = f32[32,1,128]{2,1,0:T(1,128)S(1)} async-done(((f32[32,1,128]{2,1,0:T(1,128)}), f32[32,1,128]{2,1,0:T(1,128)S(1)}, u32[]{:S(2)}, u32[]{:S(2)}) %all-to-all-start) | async-done | bytes 16416 | tf_op jit(solution)/shard_map/all_to_all | solution.py:15
  81.3 0.5 broadcast.397
  81.8 0.7 reduce.4
  82.5 0.1 reshape.293
  82.7 0.1 copy.29
  82.8 1.5 fusion.15
  84.3 0.1 copy.30
  84.4 0.0 copy-start.1
  84.4 0.1 copy.39
  84.5 0.1 convolution_multiply_fusion
  84.6 0.1 reshape.234
  84.7 0.4 all_to_all.14
  85.1 52.5 %all_to_all.20 = f32[32,1,2052]{2,1,0:T(1,128)S(1)} all-to-all(f32[32,1,2052]{2,1,0:T(1,128)S(1)} %all_to_all.14), channel_id=1, replica_groups=mesh['groups'=2,'ctx'=32,'head'=4,'rep'=2] {'ctx'}, dimensions={0} | all-to-all | bytes 525312 | tf_op jit(solution)/shard_map/all_to_all | solution.py:47
  137.7 0.2 reduce_sum.39
  137.8 0.8 broadcast_in_dim.142
  138.7 4.8 %all-to-all-start.2 = ((f32[32,1,2052]{2,1,0:T(1,128)}), f32[32,1,2052]{2,1,0:T(1,128)S(1)}, u32[]{:S(2)}, u32[]{:S(2)}) async-start(f32[32,1,2052]{2,1,0:T(1,128)} %broadcast_in_dim.142), calls=%async_computation.2 | async-start | bytes 557056 | tf_op jit(solution)/shard_map/all_to_all | solution.py:15
  143.5 0.0 copy-done.1
  143.5 0.1 fusion.23
  143.7 41.2 %all-to-all-done.2 = f32[32,1,2052]{2,1,0:T(1,128)S(1)} async-done(((f32[32,1,2052]{2,1,0:T(1,128)}), f32[32,1,2052]{2,1,0:T(1,128)S(1)}, u32[]{:S(2)}, u32[]{:S(2)}) %all-to-all-start.2) | async-done | bytes 262688 | tf_op jit(solution)/shard_map/all_to_all | solution.py:15
  184.9 0.7 reduce.2
  185.5 0.2 reshape.236
  185.7 0.4 slice.27
  186.2 0.8 divide_convert_fusion
  (13 shorter events, 0.2 us)
Async XLA Ops:
  0.0 9.5 %copy-start = (bf16[1,4,32,576]{3,2,1,0:T(8,128)(2,1)S(1)}, bf16[1,4,32,576]{3,2,1,0:T(8,128)(2,1)}, u32[]{:S(2)}) copy-start(bf16[1,4,32,576]{3,2,1,0:T(8,128)(2,1)} %param.9) | copy-start | bytes 442372
  13.9 67.4 %all-to-all-start = ((f32[32,1,128]{2,1,0:T(1,128)}), f32[32,1,128]{2,1,0:T(1,128)S(1)}, u32[]{:S(2)}, u32[]{:S(2)}) async-start(f32[32,1,128]{2,1,0:T(1,128)} %reshape.292), calls=%async_computation | async-start | bytes 32768 | tf_op jit(solution)/shard_map/all_to_all | solution.py:15
  84.4 59.1 %copy-start.1 = (bf16[1,4,576]{2,1,0:T(4,128)(2,1)S(1)}, bf16[1,4,576]{2,1,0:T(4,128)(2,1)}, u32[]{:S(2)}) copy-start(bf16[1,4,576]{2,1,0:T(4,128)(2,1)} %param.10) | copy-start | bytes 13828
  138.7 46.2 %all-to-all-start.2 = ((f32[32,1,2052]{2,1,0:T(1,128)}), f32[32,1,2052]{2,1,0:T(1,128)S(1)}, u32[]{:S(2)}, u32[]{:S(2)}) async-start(f32[32,1,2052]{2,1,0:T(1,128)} %broadcast_in_dim.142), calls=%async_computation.2 | async-start | bytes 557056 | tf_op jit(solution)/shard_map/all_to_all | solution.py:15
where the time goes:
time: 188 us; the launch traced here: 187 us
  waiting for transfers between devices  53.2 us (28%)
  blocking collectives  52.5 us (28%)
  starting transfers between devices  50.5 us (27%)
  local copies, waits for them, and re-layouts  12.2 us (6%)
  other arithmetic  11.2 us (6%)
  matrix products  7.13 us (4%)
    all_to_all x2, waiting for transfers between devices, copy_for_each(): lax.all_to_all(jnp.broadcast_to(shard[None], (size, *shard.shape)), axis,...  53.2 us
    all_to_all x1, blocking collectives, sent_and_summed(): lax.all_to_all(pieces, axis, split_axis=0, concat_axis=0, tiled=True)  52.5 us
    all_to_all x2, starting transfers between devices, copy_for_each(): lax.all_to_all(jnp.broadcast_to(shard[None], (size, *shard.shape)), axis,...  50.5 us
    unnamed x8, local copies, waits for them, and re-layouts  6.96 us
    sub x1, other arithmetic, page_layout(): limit = jnp.take(lengths, sequence_of) - page_number * page_width  4.95 us
  transfers between devices with their start and end apart: 2, of which 2 were waited for; matrix products, arithmetic and copies ran while one was open for 5% of the time, Pallas kernels for 0%

commit v1 on v0

v1 whole, which is shorter than its diff:
```python
import jax
import jax.numpy as jnp
from jax import lax
from jax.experimental import pallas as pl
from jax.experimental.pallas import tpu as pltpu
from jax.sharding import PartitionSpec as P

LATENT = 512
CHUNK = 4

score_scale = 192.0 ** (-0.5)
neg_large = -1e30


def eye(n):
    return lax.broadcasted_iota(jnp.int32, (n, n), 0) == lax.broadcasted_iota(jnp.int32, (n, n), 1)


def as_row(col):
    n = col.shape[0]
    return jnp.sum(jnp.where(eye(n), jnp.broadcast_to(col, (n, n)), 0.0), axis=0, keepdims=True)


def as_col(row):
    n = row.shape[1]
    return jnp.sum(jnp.where(eye(n), jnp.broadcast_to(row, (n, n)), 0.0), axis=1, keepdims=True)


def fetch(kv_ref, kv_buf, sems):
    copies = []
    for i in range(kv_buf.shape[0] // CHUNK):
        part = pl.ds(i * CHUNK, CHUNK)
        copy = pltpu.make_async_copy(kv_ref.at[part], kv_buf.at[part], sems.at[i])
        copy.start()
        copies.append(copy)
    return copies


def score_kernel(place_ref, counts_ref, tails_ref, slots_ref, q_ref, new_ref, kv_ref, s_ref, m_ref, own_ref, kv_buf, bias_ref, sems):
    copies = fetch(kv_ref, kv_buf, sems)
    pages, _, width = kv_buf.shape
    rows = q_ref.shape[0]
    batch = new_ref.shape[0]
    heads = rows // batch
    slots = slots_ref[...]
    slot_ids = place_ref[0] * pages + lax.broadcasted_iota(jnp.int32, (pages, slots.shape[1]), 0)
    ranks_at = lax.broadcasted_iota(jnp.int32, (pages, slots.shape[1]), 1)
    rank = jnp.sum(jnp.where(slots == slot_ids, ranks_at, 0), axis=1, keepdims=True)
    token = lax.broadcasted_iota(jnp.int32, (pages, width), 1)
    start = jnp.int32(0)
    for b in range(batch):
        count = counts_ref[0, b]
        end = start + count
        length = (count - 1) * width + tails_ref[0, b]
        inside = (rank >= start) & (rank < end)
        limit = jnp.where(inside, length - (rank - start) * width, 0)
        bias_ref[b] = jnp.where(token < limit, 0.0, neg_large)
        start = end
    q = q_ref[...]
    own = []
    for b in range(batch):
        qb = q[b * heads : (b + 1) * heads].astype(jnp.float32)
        own.append(jnp.sum(qb * new_ref[b : b + 1, :].astype(jnp.float32), axis=1, keepdims=True) * score_scale)
    own = jnp.concatenate(own, axis=0)
    best = [jnp.full((heads, width), neg_large, jnp.float32) for _ in range(batch)]
    for i, copy in enumerate(copies):
        copy.wait()
        keys = jnp.concatenate([kv_buf[i * CHUNK + j] for j in range(CHUNK)], axis=1)
        scores = jnp.dot(q, keys, preferred_element_type=jnp.float32) * score_scale
        for j in range(CHUNK):
            p = i * CHUNK + j
            for b in range(batch):
                tile = scores[b * heads : (b + 1) * heads, j * width : (j + 1) * width] + bias_ref[b, p : p + 1, :]
                best[b] = jnp.maximum(best[b], tile)
                s_ref[b * heads : (b + 1) * heads, p * width : (p + 1) * width] = tile
    top = jnp.maximum(jnp.max(jnp.concatenate(best, axis=0), axis=1, keepdims=True), own)
    m_ref[...] = jnp.broadcast_to(as_row(top)[None], m_ref.shape)
    own_ref[...] = as_row(own)


def value_kernel(place_ref, s_ref, m_ref, own_ref, new_ref, kv_ref, acc_ref, sum_ref, kv_buf, sems):
    copies = fetch(kv_ref, kv_buf, sems)
    width = kv_buf.shape[2]
    rows = s_ref.shape[0]
    batch = new_ref.shape[0]
    heads = rows // batch
    top = as_col(m_ref[0])
    own_weight = jnp.where(place_ref[0] == 0, jnp.exp(as_col(own_ref[...]) - top), 0.0)
    total = jnp.zeros((rows, width), jnp.float32)
    acc = jnp.concatenate(
        [
            own_weight[b * heads : (b + 1) * heads] * new_ref[b : b + 1, :LATENT].astype(jnp.float32)
            for b in range(batch)
        ],
        axis=0,
    )
    for i, copy in enumerate(copies):
        copy.wait()
        span = CHUNK * width
        weights = jnp.exp(s_ref[:, i * span : (i + 1) * span] - top).astype(jnp.bfloat16)
        rounded = weights.astype(jnp.float32)
        for j in range(CHUNK):
            total = total + rounded[:, j * width : (j + 1) * width]
        values = jnp.concatenate([kv_buf[i * CHUNK + j, :LATENT, :] for j in range(CHUNK)], axis=1)
        acc = acc + lax.dot_general(weights, values, (((1,), (1,)), ((), ())), preferred_element_type=jnp.float32)
    acc_ref[...] = acc
    sum_ref[...] = as_row(jnp.sum(total, axis=1, keepdims=True) + own_weight)


def scale_kernel(acc_ref, sum_ref, m_ref, all_ref, *outs):
    everything = all_ref[...]
    top = jnp.max(everything, axis=0)
    factor = jnp.exp(m_ref[0] - top)
    first = lax.broadcasted_iota(jnp.int32, factor.shape, 1) == 0
    sums = sum_ref[...] * factor
    outs[-2][...] = jnp.where(first, 0.0, sums)
    outs[-1][...] = sums[:, :1]
    col = as_col(factor)
    at = 0
    for out in outs[:-2]:
        size = out.shape[0]
        out[...] = acc_ref[at : at + size, :] * col[at : at + size]
        at += size


def finish_kernel(*refs):
    parts, rest_ref, first_ref, out_ref = refs[:-3], refs[-3], refs[-2], refs[-1]
    first = lax.broadcasted_iota(jnp.int32, rest_ref.shape, 1) == 0
    sums = as_col(jnp.where(first, first_ref[...], rest_ref[...]))
    at = 0
    for part in parts:
        size = part.shape[0]
        out_ref[at : at + size, :] = (part[...] / sums[at : at + size]).astype(out_ref.dtype)
        at += size


def local(kv_cache, queries, new_latent, page_counts, page_tails, page_slots):
    _, pages, width, depth = kv_cache.shape
    _, batch, heads, _ = queries.shape
    rows = batch * heads
    members = lax.axis_size("ctx")
    kv = jnp.swapaxes(kv_cache[0], 1, 2)
    q = queries[0].reshape(rows, depth)
    new = new_latent[0]
    place = lax.axis_index("ctx").reshape(1)
    vmem = pl.BlockSpec(memory_space=pltpu.VMEM)
    smem = pl.BlockSpec(memory_space=pltpu.SMEM)
    hbm = pl.BlockSpec(memory_space=pl.ANY)
    f32 = jnp.float32
    kv_scratch = [pltpu.VMEM((pages, depth, width), kv.dtype)]
    sems = [pltpu.SemaphoreType.DMA((pages // CHUNK,))]
    scores, tops, own = pl.pallas_call(
        score_kernel,
        out_shape=(
            jax.ShapeDtypeStruct((rows, pages * width), f32),
            jax.ShapeDtypeStruct((members, 1, rows), f32),
            jax.ShapeDtypeStruct((1, rows), f32),
        ),
        in_specs=[smem, smem, smem, vmem, vmem, vmem, hbm],
        out_specs=(vmem, vmem, vmem),
        scratch_shapes=kv_scratch + [pltpu.VMEM((batch, pages, width), f32)] + sems,
        name="scores",
    )(place, page_counts, page_tails, page_slots, q, new, kv)
    all_tops = lax.all_to_all(tops, "ctx", 0, 0, tiled=True)
    acc, sums = pl.pallas_call(
        value_kernel,
        out_shape=(jax.ShapeDtypeStruct((rows, LATENT), f32), jax.ShapeDtypeStruct((1, rows), f32)),
        in_specs=[smem, vmem, vmem, vmem, vmem, hbm],
        out_specs=(vmem, vmem),
        scratch_shapes=kv_scratch + sems,
        name="values",
    )(place, scores, tops, own, new, kv)
    pieces = 8
    size = rows // pieces
    shapes = [jax.ShapeDtypeStruct((size, LATENT), f32)] * pieces
    shapes += [jax.ShapeDtypeStruct((1, rows), f32), jax.ShapeDtypeStruct((1, 1), f32)]
    scaled = pl.pallas_call(
        scale_kernel, out_shape=tuple(shapes), in_specs=[vmem] * 4, out_specs=(vmem,) * len(shapes), name="scale"
    )(acc, sums, tops, all_tops)
    summed = lax.psum(tuple(scaled), "ctx")
    out = pl.pallas_call(
        finish_kernel,
        out_shape=jax.ShapeDtypeStruct((rows, LATENT), jnp.bfloat16),
        in_specs=[vmem] * len(shapes),
        out_specs=vmem,
        name="finish",
    )(*summed)
    return out.reshape(1, batch, heads, LATENT)


def solution(mesh):
    in_specs = (
        P(("groups", "rep"), "ctx", None, None),
        P(("groups", "rep"), None, "head", None),
        P(("groups", "rep"), None, None),
        P(("groups", "rep"), None),
        P(("groups", "rep"), None),
        P(("groups", "rep"), None),
    )
    out_specs = P(("groups", "rep"), None, "head", None)
    return jax.shard_map(local, mesh=mesh, in_specs=in_specs, out_specs=out_specs, check_vma=False)
```

time: 188 us -> 186 us (0.989)
  blocking collectives: 52.5 us -> 109 us
  waiting for transfers between devices: 53.2 us -> 17.1 us
  Pallas kernels: 0 us -> 13.6 us
  local copies, waits for them, and re-layouts: 12.2 us -> 0.6 us
  other arithmetic: 11.2 us -> 0 us
  matrix products: 7.13 us -> 0 us
  starting transfers between devices: 50.5 us -> 45.8 us
    psum x0 -> x1, blocking collectives: none -> 109 us  [local(): summed = lax.psum(tuple(scaled), 'ctx')]
    all_to_all x1 -> x0, blocking collectives: 52.5 us -> none  [sent_and_summed(): lax.all_to_all(pieces, axis, split_axis=0, concat_axis=0, tiled=True)]
    all_to_all x2 -> x1, waiting for transfers between devices: 53.2 us -> 17.1 us  [local(): all_tops = lax.all_to_all(tops, 'ctx', 0, 0, tiled=True)]
    pallas_call x0 -> x4, Pallas kernels: none -> 13.6 us  [the longest x1 4.86 us: local(): pl.pallas_call(score_kernel, out_shape=(jax.ShapeDtypeStruct((rows, pages...]
    dot_general x5 -> x0, matrix products: 7.13 us -> none  [the longest x1 2.84 us: page_partials(): jnp.einsum('phc,ptc->pht', query_pages, cache_pages, preferred_element_ty...]
    unnamed x8 -> x2, local copies, waits for them, and re-layouts: 6.96 us -> 0.6 us
    sub x1 -> x0, other arithmetic: 4.95 us -> none  [page_layout(): limit = jnp.take(lengths, sequence_of) - page_number * page_width]
    all_to_all x2 -> x1, starting transfers between devices: 50.5 us -> 45.8 us  [local(): all_tops = lax.all_to_all(tops, 'ctx', 0, 0, tiled=True)]
  transfers between devices with their start and end apart: 2 -> 1, of which waited for: 2 -> 1; matrix products, arithmetic and copies ran while one was open for 5% -> 0% of each run, Pallas kernels for 0% -> 2%
where the time goes in v1:
time: 186 us
  blocking collectives  109 us (59%)
  starting transfers between devices  45.8 us (25%)
  waiting for transfers between devices  17.1 us (9%)
  Pallas kernels  13.6 us (7%)
    psum x1, blocking collectives, local(): summed = lax.psum(tuple(scaled), 'ctx')  109 us
    all_to_all x1, starting transfers between devices, local(): all_tops = lax.all_to_all(tops, 'ctx', 0, 0, tiled=True)  45.8 us
    all_to_all x1, waiting for transfers between devices, local(): all_tops = lax.all_to_all(tops, 'ctx', 0, 0, tiled=True)  17.1 us
    pallas_call x1, Pallas kernels, local(): pl.pallas_call(score_kernel, out_shape=(jax.ShapeDtypeStruct((rows, pages...  4.86 us
    pallas_call x1, Pallas kernels, local(): pl.pallas_call(value_kernel, out_shape=(jax.ShapeDtypeStruct((rows, LATEN...  4.58 us
  transfers between devices with their start and end apart: 1, of which 1 were waited for; matrix products, arithmetic and copies ran while one was open for 0% of the time, Pallas kernels for 2%

profile of v1, /device:TPU:40, one launch (start us, length us, event | category | flops | bytes accessed | tf_op | source)
XLA Modules:
  0.0 185.7 jit_solution(12721939430229517417)
XLA Ops:
  0.0 4.9 %scores.1 = (f32[128,3072]{1,0:T(8,128)}, f32[32,1,128]{2,1,0:T(1,128)}, f32[1,128]{1,0:T(1,128)}) custom-call(s32[1]{0:T(128)} %bitcast.place_ref, s32[1,4]{1,0:T(1,128)} %counts_ref.1, s32[1,4]{1,0:T(1,128)} %tails_ref.1, s32[1,768]{1,0:T(1,128)} %slots_ref.1, bf16[128,576]{1,0:T(8,128)(2,1)} %bitcast.9, bf16[4,576]{1,0:T(4,128)(2,1)} %bitcast.10, ...), custom_call_target="tpu_custom_call" | custom-call | tf_op jit(solution)/shard_map/scores/pallas_call | solution.py:152
  4.9 45.8 %all-to-all-start = ((f32[32,1,128]{2,1,0:T(1,128)}), f32[32,1,128]{2,1,0:T(1,128)S(1)}, u32[]{:S(2)}, u32[]{:S(2)}) async-start(f32[32,1,128]{2,1,0:T(1,128)} %get-tuple-element.21.m_ref), calls=%async_computation | async-start | bytes 32768 | tf_op jit(solution)/shard_map/all_to_all | solution.py:164
  50.7 4.6 %values.1 = (f32[128,512]{1,0:T(8,128)}, f32[1,128]{1,0:T(1,128)}) custom-call(s32[1]{0:T(128)} %bitcast.place_ref, f32[128,3072]{1,0:T(8,128)} %get-tuple-element.20.s_ref, f32[32,1,128]{2,1,0:T(1,128)} %get-tuple-element.21.m_ref, f32[1,128]{1,0:T(1,128)} %get-tuple-element.22.own_ref, bf16[4,576]{1,0:T(4,128)(2,1)} %bitcast.11, bf16[24,576,128]{2,1,0:T(8,128)(2,1)} %bitcast.8), custom_call_target="tpu_custom_call" | custom-call | tf_op jit(solution)/shard_map/values/pallas_call | solution.py:165
  55.2 17.1 %all-to-all-done.all_ref = f32[32,1,128]{2,1,0:T(1,128)S(1)} async-done(((f32[32,1,128]{2,1,0:T(1,128)}), f32[32,1,128]{2,1,0:T(1,128)S(1)}, u32[]{:S(2)}, u32[]{:S(2)}) %all-to-all-start) | async-done | bytes 16416 | tf_op jit(solution)/shard_map/all_to_all | solution.py:164
  72.4 0.0 copy-start
  72.4 0.6 copy-done
  73.0 1.8 scale.1
  74.7 108.6 %all-reduce.2 = (f32[16,512]{1,0:T(8,128)}, f32[16,512]{1,0:T(8,128)}, f32[16,512]{1,0:T(8,128)}, f32[16,512]{1,0:T(8,128)}, f32[16,512]{1,0:T(8,128)}, /*index=...) all-reduce(f32[16,512]{1,0:T(8,128)} %get-tuple-element.25, ...), channel_id=1, replica_groups=mesh['groups'=2,'ctx'=32,'head'=4,'rep'=2] {'ctx'}, use_global_device_ids=true, to_apply=%region_0.0 | all-reduce | flops 65665 | bytes 525320 | tf_op jit(solution)/shard_map/psum | solution.py:180
  183.3 2.4 %finish.1 = bf16[128,512]{1,0:T(8,128)(2,1)} custom-call(f32[16,512]{1,0:T(8,128)} %get-tuple-element.35.refs_0_, f32[16,512]{1,0:T(8,128)} %get-tuple-element.36.refs_1_, f32[16,512]{1,0:T(8,128)} %get-tuple-element.37.refs_2_, f32[16,512]{1,0:T(8,128)} %get-tuple-element.38.refs_3_, f32[16,512]{1,0:T(8,128)} %get-tuple-element.39.refs_4_, ...), custom_call_target="tpu_custom_call" | custom-call | tf_op jit(solution)/shard_map/finish/pallas_call | solution.py:181
Async XLA Ops:
  4.9 67.5 %all-to-all-start = ((f32[32,1,128]{2,1,0:T(1,128)}), f32[32,1,128]{2,1,0:T(1,128)S(1)}, u32[]{:S(2)}, u32[]{:S(2)}) async-start(f32[32,1,128]{2,1,0:T(1,128)} %get-tuple-element.21.m_ref), calls=%async_computation | async-start | bytes 32768 | tf_op jit(solution)/shard_map/all_to_all | solution.py:164
  72.4 0.6 copy-start
